TPU v7x, 32 devices: a whole 2x2x4 slice. The times are simulated.
32 devices in a mesh: dp: 2 (over x), tp: 4 (over z), sp: 4 (over y, core).
Axes of the slice: x: 2, y: 2, z: 4, core: 2. Of those that a mesh axis runs over, the one named last changes fastest.
Arguments:
- tokens: bfloat16 [16, 3584], P('dp'), parts along dimension 0
- positions: int32 [16], P('dp'), parts along dimension 0
- cache_k: bfloat16 [16, 4096, 8, 256], P('dp', 'sp', 'tp'), parts along dimension 0
- cache_v: bfloat16 [16, 4096, 8, 256], P('dp', 'sp', 'tp'), parts along dimension 0
- attn_gain: bfloat16 [3584], replicated
- w_q: bfloat16 [3584, 4096], P(None, 'tp')
- w_k: bfloat16 [3584, 2048], P(None, 'tp')
- w_v: bfloat16 [3584, 2048], P(None, 'tp')
- w_o: bfloat16 [4096, 3584], P('tp')
- mlp_gain: bfloat16 [3584], replicated
- w_gate: bfloat16 [3584, 14336], P(None, 'tp')
- w_up: bfloat16 [3584, 14336], P(None, 'tp')
- w_down: bfloat16 [14336, 3584], P('tp')
Outputs:
- output 1: bfloat16 [16, 3584], P('dp'), parts along dimension 0
- output 2: bfloat16 [16, 4096, 8, 256], P('dp', 'sp', 'tp'), parts along dimension 0
- output 3: bfloat16 [16, 4096, 8, 256], P('dp', 'sp', 'tp'), parts along dimension 0
There are 2 independent parts. A program takes and returns all parts, laid end to end along the dimension named above; an argument that names none is the same for every part.
All inputs are finite; a program needn't handle non-finite values.
Results may differ from a plain program's by a relative error of at most 0.0088623.
Values sent between devices are 32-bit elements.
A program may use at most 1 GiB of HBM per device.

v0:
```python
import math
import functools
import jax
import jax.numpy as jnp
from jax import lax
from jax.experimental import pallas as pl
from jax.experimental.pallas import tpu as pltpu
from jax.sharding import PartitionSpec as P

NORM_EPS = 1e-5
ROPE_THETA = 10000.0
MESH = pl.DeviceIdType.MESH
F32 = jnp.float32
BF16 = jnp.bfloat16


def rope_tables(positions, half):
    index = lax.broadcasted_iota(jnp.int32, (positions.shape[0], half), 1).astype(F32)
    angles = positions * jnp.exp(index * (-math.log(ROPE_THETA) / half))
    turns = jnp.floor(angles * (2.0 / math.pi) + 0.5)
    rest = ((angles - turns * 1.5703125) - turns * 4.837512969970703125e-4) - turns * 7.54978995489188216e-8
    square = rest * rest
    sine = rest + rest * square * (-1.0 / 6 + square * (1.0 / 120 + square * (-1.0 / 5040 + square * (1.0 / 362880))))
    cosine = 1.0 + square * (-0.5 + square * (1.0 / 24 + square * (-1.0 / 720 + square * (1.0 / 40320 - square * (1.0 / 3628800)))))
    quadrant = turns.astype(jnp.int32) & 3
    swap = (quadrant & 1) == 1
    cos_value = jnp.where(swap, sine, cosine)
    sin_value = jnp.where(swap, cosine, sine)
    return (jnp.where((quadrant == 1) | (quadrant == 2), -cos_value, cos_value),
            jnp.where(quadrant >= 2, -sin_value, sin_value))


def scaled_norm(wide, gain_ref):
    inv_rms = lax.rsqrt(jnp.mean(wide * wide, axis=-1, keepdims=True) + NORM_EPS)
    gain = gain_ref[...].astype(F32)
    pieces = [(wide[:, i * 128:(i + 1) * 128] * inv_rms * gain[i:i + 1]).astype(BF16) for i in range(wide.shape[1] // 128)]
    return jnp.concatenate(pieces, axis=1)


def exchange(axis, source, slots_ref, send_sem, recv_sem, unsent):
    me = lax.axis_index(axis)
    size = slots_ref[0].shape[0]
    dst, cols = slots_ref
    copies = []
    for i in range(size - 1):
        down, up = size - 1 - i, i
        low = jnp.where(down > me, down, down - 1)
        high = jnp.where(up < me, up, up + 1)
        peer = jnp.where(me < size // 2, low, high)
        copies.append((
            pltpu.make_async_remote_copy(
                src_ref=source, dst_ref=dst.at[(me,) + cols], send_sem=send_sem.at[peer], recv_sem=recv_sem.at[me],
                device_id={axis: peer}, device_id_type=MESH),
            pltpu.make_async_remote_copy(
                src_ref=source, dst_ref=dst.at[(peer,) + cols], send_sem=send_sem.at[peer], recv_sem=recv_sem.at[peer],
                device_id={axis: peer}, device_id_type=MESH)))
        copies[-1][0].start()
    unsent.extend(sent for sent, _ in copies)
    return copies


def finish(copies):
    for _, arriving in copies:
        arriving.wait_recv()


def added(slots_ref, cols):
    total = slots_ref[0, :, cols]
    for t in range(1, slots_ref.shape[0]):
        total = total + slots_ref[t, :, cols]
    return total


def layer_kernel(sp_size, tp_size, cuts, positions, tokens, attn_gain, mlp_gain, wq, wk, wv, ck, cv, wo, wg, wu, wd,
                 kbuf, vbuf, k_row, v_row, out_ref,
                 pos_ref, tok_ref, tok_cols, ag_ref, mg_ref, wqkv_buf, wo_buf, wgu_buf, wd_buf,
                 part0, r0, q3, k3, v3, kq3, vq3, o3, m3, l3, part1, r1, att, part2, r2, part3, r3, part4, r4, part5, r5, part6, r6,
                 psem, wsem, ksem, vsem, osem, gsem, dsem, ssem0, rsem0, ssem1, rsem1, ssem, rsem):
    rows, depth = tokens.shape
    _, local_slots, kv_local, head_dim = ck.shape
    slots = local_slots * sp_size
    q_width, kv_width = wq.shape[1], wk.shape[1]
    heads = q_width // head_dim
    group = heads // kv_local
    half = head_dim // 2
    width = depth // sp_size
    q_cols, kv_cols = q_width // sp_size, kv_width // sp_size
    flat = local_slots * kv_local
    sp, tp = lax.axis_index("sp"), lax.axis_index("tp")
    first_slot = sp * local_slots
    start = pl.multiple_of(sp * width, 128)
    my_cols = pl.ds(start, width)
    cuts, mid_cuts = cuts
    pieces = [pl.ds(a, b - a) for a, b in zip((0,) + cuts[:-1], cuts)]
    mid_pieces = [pl.ds(a, b - a) for a, b in zip((0,) + mid_cuts[:-1], mid_cuts)]
    unsent = []

    barrier = pltpu.get_barrier_semaphore()
    for axis, me, size in (("sp", sp, sp_size), ("tp", tp, tp_size)):
        for d in range(1, size):
            pl.semaphore_signal(barrier, inc=1, device_id={axis: lax.rem(me + d, size)}, device_id_type=MESH)

    small = [pltpu.make_async_copy(tokens, tok_ref, psem.at[0]), pltpu.make_async_copy(attn_gain, ag_ref, psem.at[1]),
             pltpu.make_async_copy(positions, pos_ref, psem.at[2]), pltpu.make_async_copy(mlp_gain, mg_ref, psem.at[3]),
             pltpu.make_async_copy(tokens.at[:, my_cols], tok_cols, psem.at[4])]
    q_part = pl.ds(pl.multiple_of(sp * q_cols, 128), q_cols)
    kv_part = pl.ds(pl.multiple_of(sp * kv_cols, 128), kv_cols)
    qkv_loads = [pltpu.make_async_copy(wq.at[:, q_part], wqkv_buf.at[:, pl.ds(0, q_cols)], wsem.at[0]),
                 pltpu.make_async_copy(wk.at[:, kv_part], wqkv_buf.at[:, pl.ds(q_cols, kv_cols)], wsem.at[1]),
                 pltpu.make_async_copy(wv.at[:, kv_part], wqkv_buf.at[:, pl.ds(q_cols + kv_cols, kv_cols)], wsem.at[2])]
    k_flat, v_flat = ck.reshape(rows, flat, head_dim), cv.reshape(rows, flat, head_dim)
    k_in = [pltpu.make_async_copy(k_flat.at[b], kbuf.at[b], ksem.at[b]) for b in range(rows)]
    v_in = [pltpu.make_async_copy(v_flat.at[b], vbuf.at[b], vsem.at[b]) for b in range(rows)]
    o_load = pltpu.make_async_copy(wo.at[:, my_cols], wo_buf, osem)
    gate_loads, down_loads = [], []
    for i, piece in enumerate(mid_pieces):
        cols = pl.ds(start + piece.start, piece.size)
        gate_loads.append([
            pltpu.make_async_copy(wg.at[:, cols], wgu_buf.at[:, pl.ds(2 * piece.start, piece.size)], gsem.at[i, 0]),
            pltpu.make_async_copy(wu.at[:, cols], wgu_buf.at[:, pl.ds(2 * piece.start + piece.size, piece.size)], gsem.at[i, 1])])
        down_loads.append([
            pltpu.make_async_copy(wd.at[pl.ds(s * width + piece.start, piece.size), my_cols],
                                  wd_buf.at[pl.ds(sp_size * piece.start + s * piece.size, piece.size), :], dsem.at[i, s])
            for s in range(sp_size)])
    for copy in small[:2] + qkv_loads + small[2:]:
        copy.start()
    for b in range(rows):
        k_in[b].start()
        v_in[b].start()
    o_load.start()
    for loads in gate_loads + down_loads:
        for copy in loads:
            copy.start()

    with jax.named_scope("small"):
        for copy in small[:2]:
            copy.wait()
        normed = scaled_norm(tok_ref[...].astype(F32), ag_ref)
    with jax.named_scope("wait_qkv"):
        for copy in qkv_loads:
            copy.wait()
    with jax.named_scope("qkv"):
        mine = jnp.dot(normed, wqkv_buf[...], preferred_element_type=F32)
        part0[...] = mine
    with jax.named_scope("barrier"):
        pl.semaphore_wait(barrier, sp_size + tp_size - 2)
    moved = exchange("sp", part0, (r0, ()), ssem0, rsem0, unsent)
    r0[sp] = mine

    for copy in small[2:]:
        copy.wait()
    row = lax.broadcasted_iota(jnp.int32, (rows, half), 0)
    position_rows = jnp.zeros((rows, half), F32)
    for b in range(rows):
        position_rows = jnp.where(row == b, pos_ref[b].astype(F32), position_rows)
    cos_table, sin_table = rope_tables(position_rows, half)
    scale = 1.0 / math.sqrt(head_dim)
    side = part1.shape[1]
    tall = side * heads
    column = lax.broadcasted_iota(jnp.int32, (tall, flat), 1)
    line = lax.broadcasted_iota(jnp.int32, (tall, flat), 0)
    own_head = lax.rem(column, kv_local) == lax.rem(line, heads) // group
    member = line // heads
    value_member = lax.broadcasted_iota(jnp.int32, (tall, head_dim), 0) // heads
    slot_ids = first_slot + column // kv_local
    with jax.named_scope("p0"):
        finish(moved)

    def rotate(a, b):
        return a * cos_table - b * sin_table, b * cos_table + a * sin_table

    def gathered(offset, size, index):
        s, at = index * half // size, index * half % size
        return r0[s, :, offset + at:offset + at + half]

    for j in range(heads):
        a, b = rotate(gathered(0, q_cols, 2 * j), gathered(0, q_cols, 2 * j + 1))
        q3[:, j, 0:half] = a
        q3[:, j, half:head_dim] = b
    for j in range(kv_local):
        a, b = rotate(gathered(q_cols, kv_cols, 2 * j), gathered(q_cols, kv_cols, 2 * j + 1))
        k3[:, j, 0:half] = a
        k3[:, j, half:head_dim] = b
        v3[:, j, 0:half] = gathered(q_cols + kv_cols, kv_cols, 2 * j)
        v3[:, j, half:head_dim] = gathered(q_cols + kv_cols, kv_cols, 2 * j + 1)
    k_row[...] = k3[...].astype(BF16)
    v_row[...] = v3[...].astype(BF16)

    k_rounded, v_rounded = k_row[...].astype(F32), v_row[...].astype(F32)
    for j in range(heads):
        kq3[:, j, :] = k_rounded[:, j // group, :]
        vq3[:, j, :] = v_rounded[:, j // group, :]

    sends = []
    lane = lax.broadcasted_iota(jnp.int32, (side, 128), 1) // 16
    for g in range(rows // side):
        members = range(g * side, (g + 1) * side)
        with jax.named_scope(f"kv{g}"):
            for b in members:
                k_in[b].wait()
                v_in[b].wait()
        target = jnp.zeros((tall, flat), jnp.int32)
        limit = jnp.zeros((tall, flat), jnp.int32)
        for i, b in enumerate(members):
            position = pos_ref[b]
            target = jnp.where(member == i, lax.rem(position, slots), target)
            limit = jnp.where(member == i, jnp.where(position >= slots - 1, slots, position), limit)
        queries = jnp.concatenate([q3[b] for b in members], axis=0).astype(BF16)
        new_key = jnp.concatenate([kq3[b] for b in members], axis=0)
        new_value = jnp.concatenate([vq3[b] for b in members], axis=0)
        new_score = jnp.sum(queries.astype(F32) * new_key, axis=1, keepdims=True) * scale
        scores = jnp.zeros((tall, flat), F32)
        for i, b in enumerate(members):
            product = lax.dot_general(queries, kbuf[b], (((1,), (1,)), ((), ())), preferred_element_type=F32)
            scores = jnp.where(member == i, product, scores)
        fresh = slot_ids == target
        valid = own_head & (slot_ids <= limit)
        scores = jnp.where(valid, jnp.where(fresh, new_score, scores * scale), -jnp.inf)
        top = jnp.max(scores, axis=1, keepdims=True)
        weights = jnp.exp(scores - jnp.where(top == -jnp.inf, 0.0, top))
        new_weight = jnp.sum(jnp.where(fresh, weights, 0.0), axis=1, keepdims=True)
        stored = (weights * jnp.where(fresh, 0.0, 1.0)).astype(BF16)
        value = jnp.zeros((tall, head_dim), F32)
        for i, b in enumerate(members):
            product = jnp.dot(stored, vbuf[b], preferred_element_type=F32)
            value = jnp.where(value_member == i, product, value)
        value = value + new_weight.astype(BF16).astype(F32) * new_value
        top = jnp.broadcast_to(top, (tall, 128))
        size = jnp.broadcast_to(jnp.sum(weights, axis=1, keepdims=True), (tall, 128))
        for i, b in enumerate(members):
            own = slice(i * heads, (i + 1) * heads)
            o3[b], m3[b], l3[b] = value[own], top[own], size[own]
        rows_here = pl.ds(g * side, side)
        stats = jnp.zeros((side, 128), F32)
        for j in range(heads):
            part1[g, :, j * head_dim:(j + 1) * head_dim] = o3[rows_here, j, :]
            stats = jnp.where(lane == j, m3[rows_here, j, :], stats)
            stats = jnp.where(lane == heads + j, l3[rows_here, j, :], stats)
        part1[g, :, q_width:q_width + 128] = stats
        sends.append(exchange("sp", part1.at[g], (r1, (g,)), ssem1.at[g], rsem1.at[g], unsent))
        r1[sp, g] = part1[g]

    for g, copies in enumerate(sends):
        with jax.named_scope(f"p1_{g}"):
            finish(copies)
        stats = [r1[s, g, :, q_width:q_width + 128] for s in range(sp_size)]
        for j in range(heads):
            tops = [t[:, j * 16:j * 16 + 1] for t in stats]
            best = functools.reduce(jnp.maximum, tops)
            numerator = jnp.zeros((side, head_dim), F32)
            denominator = jnp.zeros((side, 1), F32)
            for s in range(sp_size):
                factor = jnp.exp(tops[s] - best)
                numerator = numerator + r1[s, g, :, j * head_dim:(j + 1) * head_dim] * factor
                denominator = denominator + stats[s][:, (heads + j) * 16:(heads + j) * 16 + 1] * factor
            att[g * side:(g + 1) * side, j * head_dim:(j + 1) * head_dim] = numerator / denominator
    attended = att[...].astype(BF16)

    def pass_on(axis, me, source, slots_ref, phase, i, piece):
        copies = exchange(axis, source.at[:, piece], (slots_ref, (slice(None), piece)), ssem.at[phase, i], rsem.at[phase, i], unsent)
        slots_ref[me, :, piece] = source[:, piece]
        return copies

    def settle(base, sent, slots_ref, target, target_slots, phase):
        passed = []
        for i, piece in enumerate(pieces):
            with jax.named_scope(f"tp{phase}_{i}"):
                finish(sent[i])
            target[:, piece] = (base[:, piece] + added(slots_ref, piece)).astype(BF16).astype(F32)
            passed.append(pass_on("sp", sp, target, target_slots, phase, i, piece))
        return passed

    o_load.wait()
    sent = []
    for i, piece in enumerate(pieces):
        with jax.named_scope(f"fence_o{i}"):
            unsent.pop(0).wait_send()
        part2[:, piece] = jnp.dot(attended, wo_buf[:, piece], preferred_element_type=F32)
        sent.append(pass_on("tp", tp, part2, r2, 0, i, piece))
    part6[...] = tok_cols[...].astype(F32)
    passed = settle(part6, sent, r2, part3, r3, 1)
    with jax.named_scope("p3"):
        for copies in passed:
            finish(copies)
    normed = scaled_norm(jnp.concatenate([r3[s] for s in range(sp_size)], axis=1), mg_ref)

    moved = []
    for i, piece in enumerate(mid_pieces):
        with jax.named_scope(f"wait_gate{i}"):
            for copy in gate_loads[i]:
                copy.wait()
        both = jnp.dot(normed, wgu_buf[:, 2 * piece.start:2 * (piece.start + piece.size)], preferred_element_type=F32)
        gate, up = both[:, :piece.size], both[:, piece.size:]
        part4[:, piece] = (gate * jax.nn.sigmoid(gate) * up).astype(BF16).astype(F32)
        moved.append(pass_on("sp", sp, part4, r4, 2, i, piece))
    total = None
    for i, piece in enumerate(mid_pieces):
        with jax.named_scope(f"p4_{i}"):
            for copy in down_loads[i]:
                copy.wait()
            finish(moved[i])
        left = jnp.concatenate([r4[s, :, piece] for s in range(sp_size)], axis=1).astype(BF16)
        down = pl.ds(sp_size * piece.start, sp_size * piece.size)
        if i + 1 < len(mid_pieces):
            product = jnp.dot(left, wd_buf[down, :], preferred_element_type=F32)
            total = product if total is None else total + product
            part5[...] = total
    sent = []
    for i, piece in enumerate(pieces):
        with jax.named_scope(f"fence{i}"):
            unsent.pop(0).wait_send()
        part5[:, piece] = part5[:, piece] + jnp.dot(left, wd_buf[down, piece], preferred_element_type=F32)
        sent.append(pass_on("tp", tp, part5, r5, 3, i, piece))
    passed = settle(part3, sent, r5, part6, r6, 4)
    with jax.named_scope("p6"):
        for copies in passed:
            finish(copies)
    for copy in unsent:
        copy.wait_send()
    out_ref[...] = jnp.concatenate([r6[s] for s in range(sp_size)], axis=1).astype(BF16)


def write_kernel(sp_size, pos_ref, k_in, v_in, k_row, v_row, out_in, new_k, new_v, out_ref, kbuf, vbuf, ksem, vsem, osem):
    rows, local_slots, kv_local, head_dim = new_k.shape
    flat = local_slots * kv_local
    tile = 16
    first_slot = lax.axis_index("sp") * local_slots
    copies = [pltpu.make_async_copy(out_in, out_ref, osem)]
    k_flat, v_flat = new_k.reshape(rows, flat, head_dim), new_v.reshape(rows, flat, head_dim)
    for b in range(rows):
        target = lax.rem(pos_ref[b], local_slots * sp_size) - first_slot

        @pl.when((target >= 0) & (target < local_slots))
        def _():
            base = pl.multiple_of((target * kv_local) // tile * tile, tile)
            at = target * kv_local - base
            row = lax.broadcasted_iota(jnp.int32, (tile, head_dim), 0)
            for buf, fresh in ((kbuf, k_row), (vbuf, v_row)):
                block = buf[b, pl.ds(base, tile), :].astype(F32)
                pair = fresh[b].astype(F32)
                for h in range(kv_local):
                    block = jnp.where(row == at + h, pair[h:h + 1], block)
                buf[b, pl.ds(base, tile), :] = block.astype(BF16)

    for b in range(rows):
        copies.append(pltpu.make_async_copy(kbuf.at[b], k_flat.at[b], ksem.at[b]))
        copies.append(pltpu.make_async_copy(vbuf.at[b], v_flat.at[b], vsem.at[b]))
    for copy in copies:
        copy.start()
    for copy in copies:
        copy.wait()


def solution(mesh):
    sp_size, tp_size = mesh.shape["sp"], mesh.shape["tp"]
    cache_spec = P("dp", "sp", "tp", None)
    row_spec = P("dp", None)
    col_spec = P(None, "tp")
    in_specs = (row_spec, P("dp"), cache_spec, cache_spec, P(None), col_spec, col_spec, col_spec, P("tp", None), P(None), col_spec, col_spec, P("tp", None))
    out_specs = (row_spec, cache_spec, cache_spec)

    def local_step(tokens, positions, cache_k, cache_v, attn_gain, w_q, w_k, w_v, w_o, mlp_gain, w_gate, w_up, w_down):
        rows, depth = tokens.shape
        _, local_slots, kv_local, head_dim = cache_k.shape
        q_width, kv_width = w_q.shape[1], w_k.shape[1]
        heads = q_width // head_dim
        width = depth // sp_size
        cuts = ((512, width), (512, width))
        groups = 2
        flat_shape = (rows, local_slots * kv_local, head_dim)
        vmem = pl.BlockSpec(memory_space=pltpu.VMEM)
        hbm = pl.BlockSpec(memory_space=pltpu.HBM)
        dma = pltpu.SemaphoreType.DMA
        in_hbm = functools.partial(pltpu.with_memory_space_constraint, memory_space=pltpu.HBM)
        in_vmem = functools.partial(pltpu.with_memory_space_constraint, memory_space=pltpu.VMEM)
        f32 = lambda *shape: pltpu.VMEM(shape, F32)
        bf16 = lambda *shape: pltpu.VMEM(shape, BF16)
        qkv_cols = (q_width + 2 * kv_width) // sp_size
        packed = (groups, rows // groups, q_width + 128)
        k_here, v_here, k_row, v_row, out_here = pl.pallas_call(
            functools.partial(layer_kernel, sp_size, tp_size, cuts),
            out_shape=[bf16(*flat_shape), bf16(*flat_shape), bf16(rows, kv_local, head_dim), bf16(rows, kv_local, head_dim), bf16(rows, depth)],
            in_specs=[hbm] * 13,
            out_specs=[vmem] * 5,
            scratch_shapes=[
                pltpu.SMEM((rows,), jnp.int32), bf16(rows, depth), bf16(rows, width), bf16(depth // 128, 128), bf16(depth // 128, 128),
                bf16(depth, qkv_cols), bf16(q_width, width), bf16(depth, 2 * width), bf16(w_down.shape[0], width),
                f32(rows, qkv_cols), f32(sp_size, rows, qkv_cols),
                f32(rows, heads, head_dim), f32(rows, kv_local, head_dim), f32(rows, kv_local, head_dim),
                f32(rows, heads, head_dim), f32(rows, heads, head_dim), f32(rows, heads, head_dim), f32(rows, heads, 128), f32(rows, heads, 128),
                f32(*packed), f32(sp_size, *packed), f32(rows, q_width),
                f32(rows, width), f32(tp_size, rows, width), f32(rows, width), f32(sp_size, rows, width),
                f32(rows, width), f32(sp_size, rows, width), f32(rows, width), f32(tp_size, rows, width),
                f32(rows, width), f32(sp_size, rows, width),
                dma((5,)), dma((3,)), dma((rows,)), dma((rows,)), dma, dma((2, 2)), dma((2, sp_size)),
                dma((sp_size,)), dma((sp_size,)), dma((groups, sp_size)), dma((groups, sp_size)),
                dma((5, 2, sp_size)), dma((5, 2, sp_size)),
            ],
            compiler_params=pltpu.CompilerParams(vmem_limit_bytes=46 * 2 ** 20, collective_id=0, has_side_effects=True),
            cost_estimate=pl.CostEstimate(flops=10 ** 9, bytes_accessed=42 * 10 ** 6, transcendentals=0),
            name="layer",
        )(*map(in_hbm, (positions, tokens, attn_gain.reshape(depth // 128, 128), mlp_gain.reshape(depth // 128, 128),
                        w_q, w_k, w_v, cache_k, cache_v, w_o, w_gate, w_up, w_down)))

        new_k, new_v, out, _, _ = pl.pallas_call(
            functools.partial(write_kernel, sp_size),
            out_shape=[pltpu.HBM(cache_k.shape, BF16), pltpu.HBM(cache_v.shape, BF16), pltpu.HBM((rows, depth), BF16),
                       bf16(*flat_shape), bf16(*flat_shape)],
            in_specs=[pl.BlockSpec(memory_space=pltpu.SMEM)] + [vmem] * 5,
            out_specs=[hbm] * 3 + [vmem] * 2,
            scratch_shapes=[dma((rows,)), dma((rows,)), dma],
            input_output_aliases={1: 3, 2: 4},
            compiler_params=pltpu.CompilerParams(vmem_limit_bytes=4 * 2 ** 20),
            cost_estimate=pl.CostEstimate(flops=10 ** 9, bytes_accessed=17 * 10 ** 6, transcendentals=0),
            name="write",
        )(positions, *map(in_vmem, (k_here, v_here, k_row, v_row, out_here)))
        return out, new_k, new_v

    return jax.shard_map(local_step, mesh=mesh, in_specs=in_specs, out_specs=out_specs, check_vma=False)
```

profile of v0, /device:TPU:0, one launch (start us, length us, event | category | flops | bytes accessed | tf_op | source)
XLA Modules:
  0.0 44.3 jit_solution(18283835883519589759)
XLA Ops:
  0.6 0.0 copy-start
  0.6 37.0 %layer.1 = (bf16[8,2048,256]{2,1,0:T(8,128)(2,1)S(1)}, bf16[8,2048,256]{2,1,0:T(8,128)(2,1)S(1)}, bf16[8,2,256]{2,1,0:T(2,128)(2,1)S(1)}, bf16[8,2,256]{2,1,0:T(2,128)(2,1)S(1)}, bf16[8,3584]{1,0:T(8,128)(2,1)S(1)}) custom-call(s32[8]{0:T(128)} %pos_ref.1, bf16[8,3584]{1,0:T(8,128)(2,1)} %tokens.1, bf16[28,128]{1,0:T(8,128)(2,1)} %bitcast.2, ...), custom_call_target="tpu_custom_call" | custom-call | flops 1000000000 | bytes 42000000 | tf_op jit(solution)/shard_map/layer/pallas_call | solution.py:380
  37.6 0.0 copy-done
  37.7 6.7 %write.1 = (bf16[8,1024,2,256]{3,2,1,0:T(2,128)(2,1)}, bf16[8,1024,2,256]{3,2,1,0:T(2,128)(2,1)}, bf16[8,3584]{1,0:T(8,128)(2,1)}, bf16[8,2048,256]{2,1,0:T(8,128)(2,1)S(1)}, bf16[8,2048,256]{2,1,0:T(8,128)(2,1)S(1)}) custom-call(s32[8]{0:T(128)S(1)} %copy-done, ...), custom_call_target="tpu_custom_call", output_to_operand_aliasing={{3}: (1, {}), {4}: (2, {})} | custom-call | flops 1000000000 | bytes 17000000 | tf_op jit(solution)/shard_map/write/pallas_call | solution.py:405
Async XLA Ops:
  0.6 37.0 %copy-start = (s32[8]{0:T(128)S(1)}, s32[8]{0:T(128)}, u32[]{:S(2)}) copy-start(s32[8]{0:T(128)} %pos_ref.1) | copy-start | bytes 100
where the time goes:
time: 44.5 us; the launch traced here: 44.3 us
  Pallas kernels  43.7 us (98%)
  between operations  0.66 us (1%)
    pallas_call x1, Pallas kernels, local_step(): pl.pallas_call(functools.partial(layer_kernel, sp_size, tp_size, cuts), o...  37 us
    pallas_call x1, Pallas kernels, local_step(): pl.pallas_call(functools.partial(write_kernel, sp_size), out_shape=[pltpu...  6.66 us

commit v1 on v0

--- a/solution.py
+++ b/solution.py
@@ -273,8 +273,6 @@
     o_load.wait()
     sent = []
     for i, piece in enumerate(pieces):
-        with jax.named_scope(f"fence_o{i}"):
-            unsent.pop(0).wait_send()
         part2[:, piece] = jnp.dot(attended, wo_buf[:, piece], preferred_element_type=F32)
         sent.append(pass_on("tp", tp, part2, r2, 0, i, piece))
     part6[...] = tok_cols[...].astype(F32)
@@ -307,8 +305,6 @@
             part5[...] = total
     sent = []
     for i, piece in enumerate(pieces):
-        with jax.named_scope(f"fence{i}"):
-            unsent.pop(0).wait_send()
         part5[:, piece] = part5[:, piece] + jnp.dot(left, wd_buf[down, piece], preferred_element_type=F32)
         sent.append(pass_on("tp", tp, part5, r5, 3, i, piece))
     passed = settle(part3, sent, r5, part6, r6, 4)
@@ -325,7 +321,7 @@
     flat = local_slots * kv_local
     tile = 16
     first_slot = lax.axis_index("sp") * local_slots
-    copies = [pltpu.make_async_copy(out_in, out_ref, osem)]
+    copies = [[pltpu.make_async_copy(out_in, out_ref, osem)]]
     k_flat, v_flat = new_k.reshape(rows, flat, head_dim), new_v.reshape(rows, flat, head_dim)
     for b in range(rows):
         target = lax.rem(pos_ref[b], local_slots * sp_size) - first_slot
@@ -342,13 +338,14 @@
                     block = jnp.where(row == at + h, pair[h:h + 1], block)
                 buf[b, pl.ds(base, tile), :] = block.astype(BF16)
 
-    for b in range(rows):
-        copies.append(pltpu.make_async_copy(kbuf.at[b], k_flat.at[b], ksem.at[b]))
-        copies.append(pltpu.make_async_copy(vbuf.at[b], v_flat.at[b], vsem.at[b]))
-    for copy in copies:
+        copies.append([pltpu.make_async_copy(kbuf.at[b], k_flat.at[b], ksem.at[b]), pltpu.make_async_copy(vbuf.at[b], v_flat.at[b], vsem.at[b])])
+        for copy in copies[b]:
+            copy.start()
+    for copy in copies[rows]:
         copy.start()
-    for copy in copies:
-        copy.wait()
+    for pair in copies:
+        for copy in pair:
+            copy.wait()
 
 
 def solution(mesh):

time: 44.5 us -> 44.4 us (level)
  no operation moved by 1% of the time
where the time goes in v1:
time: 44.4 us; the launch traced here: 44.2 us
  Pallas kernels  43.5 us (98%)
  between operations  0.66 us (1%)
    pallas_call x1, Pallas kernels, local_step(): pl.pallas_call(functools.partial(layer_kernel, sp_size, tp_size, cuts), o...  37 us
    pallas_call x1, Pallas kernels, local_step(): pl.pallas_call(functools.partial(write_kernel, sp_size), out_shape=[pltpu...  6.54 us

profile of v1, /device:TPU:0, one launch (start us, length us, event | category | flops | bytes accessed | tf_op | source)
XLA Modules:
  0.0 44.2 jit_solution(17504819904122666291)
XLA Ops:
  0.6 0.0 copy-start
  0.6 37.0 %layer.1 = (bf16[8,2048,256]{2,1,0:T(8,128)(2,1)S(1)}, bf16[8,2048,256]{2,1,0:T(8,128)(2,1)S(1)}, bf16[8,2,256]{2,1,0:T(2,128)(2,1)S(1)}, bf16[8,2,256]{2,1,0:T(2,128)(2,1)S(1)}, bf16[8,3584]{1,0:T(8,128)(2,1)S(1)}) custom-call(s32[8]{0:T(128)} %pos_ref.1, bf16[8,3584]{1,0:T(8,128)(2,1)} %tokens.1, bf16[28,128]{1,0:T(8,128)(2,1)} %bitcast.2, ...), custom_call_target="tpu_custom_call" | custom-call | flops 1000000000 | bytes 42000000 | tf_op jit(solution)/shard_map/layer/pallas_call | solution.py:377
  37.6 0.0 copy-done
  37.7 6.5 %write.1 = (bf16[8,1024,2,256]{3,2,1,0:T(2,128)(2,1)}, bf16[8,1024,2,256]{3,2,1,0:T(2,128)(2,1)}, bf16[8,3584]{1,0:T(8,128)(2,1)}, bf16[8,2048,256]{2,1,0:T(8,128)(2,1)S(1)}, bf16[8,2048,256]{2,1,0:T(8,128)(2,1)S(1)}) custom-call(s32[8]{0:T(128)S(1)} %copy-done, ...), custom_call_target="tpu_custom_call", output_to_operand_aliasing={{3}: (1, {}), {4}: (2, {})} | custom-call | flops 1000000000 | bytes 17000000 | tf_op jit(solution)/shard_map/write/pallas_call | solution.py:402
Async XLA Ops:
  0.6 37.0 %copy-start = (s32[8]{0:T(128)S(1)}, s32[8]{0:T(128)}, u32[]{:S(2)}) copy-start(s32[8]{0:T(128)} %pos_ref.1) | copy-start | bytes 100
